TPU v7x, 32 devices: a whole 2x2x4 slice. The times are simulated.
32 devices in a mesh: grp: 2 (over y), gx: 4 (over z), gy: 2 (over x), gz: 2 (over core).
Axes of the slice: x: 2, y: 2, z: 4, core: 2. Of those that a mesh axis runs over, the one named last changes fastest.
Arguments:
- design: int32 [16, 16, 256], P(('grp', 'gx'), 'gy', 'gz'), parts along dimension 0, may hold values from 0 to 15
- supports: int32 [16, 16, 256], P(('grp', 'gx'), 'gy', 'gz'), parts along dimension 0, may hold values 0 or 1
- body_load: float32 [12, 3, 8, 16, 256], P('grp', None, 'gx', 'gy', 'gz'), parts along dimension 0, may hold values from -6 to 6
- start: float32 [12, 3, 8, 16, 256], P('grp', None, 'gx', 'gy', 'gz'), parts along dimension 0, may hold values from -1.8 to 1.8
- load_nodes: int32 [12, 16], P('grp'), parts along dimension 0, may hold values from 0 to 32767
- load_values: float32 [12, 16, 3], P('grp'), parts along dimension 0, may hold values from -24 to 24
Outputs:
- solution: float32 [12, 3, 8, 16, 256], P('grp', None, 'gx', 'gy', 'gz'), parts along dimension 0
- residual: float32 [12, 3, 8, 16, 256], P('grp', None, 'gx', 'gy', 'gz'), parts along dimension 0
There are 2 independent parts, one for each index of `grp`. A program takes and returns all parts, laid end to end along the dimension named above; each array names one. Nothing has to cross between parts.
Inputs may be any that keep to these rules, and one draw needn't show every extreme that they name: `supports`: 1 where all three displacements of the node are held fixed. `load_nodes`: flat index (i * 16 + j) * 256 + k of a loaded node; a node may be named several times.
All inputs are finite; a program needn't handle non-finite values. No bound on the sum of `supports` on one device may be relied on, other than what follows from the above.
Results may differ from a plain program's by a relative error of at most 0.0003.
Values sent between devices are 32-bit elements; how exact they have to be, the bound alone decides.
A program may use at most 64 MiB of HBM per device.

v0:
```python
import functools
import itertools

import jax
import jax.numpy as jnp
import numpy as np
from jax import lax
from jax.experimental import pallas as pl
from jax.experimental.pallas import tpu as pltpu
from jax.sharding import PartitionSpec as P

LEVELS = 16
AXES = ("gx", "gy", "gz")
MESH = pl.DeviceIdType.MESH
soft_modulus = 0.05
poisson_ratio = 0.3
DIRECTIONS = [d for d in itertools.product((-1, 0, 1), repeat=3) if d != (0, 0, 0)]


def corner_list():
    return [(first, second, third) for first in (0, 1) for second in (0, 1) for third in (0, 1)]


def element_matrix():
    lame_first = poisson_ratio / ((1.0 + poisson_ratio) * (1.0 - 2.0 * poisson_ratio))
    shear_modulus = 1.0 / (2.0 * (1.0 + poisson_ratio))
    elastic = np.zeros((6, 6))
    elastic[:3, :3] = lame_first
    for axis_dim in range(3):
        elastic[axis_dim, axis_dim] += 2.0 * shear_modulus
        elastic[3 + axis_dim, 3 + axis_dim] = shear_modulus
    gauss_points = [0.5 - 0.5 / np.sqrt(3.0), 0.5 + 0.5 / np.sqrt(3.0)]
    corners = corner_list()
    matrix_total = np.zeros((24, 24))
    for first_point in gauss_points:
        for second_point in gauss_points:
            for third_point in gauss_points:
                points = (first_point, second_point, third_point)
                strain = np.zeros((6, 24))
                for number, corner in enumerate(corners):
                    values = [
                        points[axis_dim] if corner[axis_dim] else 1.0 - points[axis_dim]
                        for axis_dim in range(3)
                    ]
                    slopes = [1.0 if corner[axis_dim] else -1.0 for axis_dim in range(3)]
                    grad_first = slopes[0] * values[1] * values[2]
                    grad_second = values[0] * slopes[1] * values[2]
                    grad_third = values[0] * values[1] * slopes[2]
                    column = 3 * number
                    strain[0, column] = grad_first
                    strain[1, column + 1] = grad_second
                    strain[2, column + 2] = grad_third
                    strain[3, column] = grad_second
                    strain[3, column + 1] = grad_first
                    strain[4, column + 1] = grad_third
                    strain[4, column + 2] = grad_second
                    strain[5, column] = grad_third
                    strain[5, column + 2] = grad_first
                matrix_total = matrix_total + strain.T @ elastic @ strain / 8.0
    return matrix_total


def mode_matrix():
    matrix = element_matrix()
    pair = np.array([[1.0, 1.0], [-1.0, 1.0]])
    basis = np.kron(np.kron(np.kron(pair, pair), pair), np.eye(3))
    inverse = np.linalg.inv(basis)
    modes = inverse.T @ matrix @ inverse
    modes[np.abs(modes) < 1e-9] = 0.0
    return float(np.float32(matrix[0, 0])), modes


def triangle(count):
    return [(i, j) for i in range(count) for j in range(i, count)]


def spd_factor(entry, count):
    lower, inverse = {}, []
    work = {(i, j): entry(j, i) for i in range(count) for j in range(i + 1)}
    for k in range(count):
        inverse.append(1.0 / work[k, k])
        for i in range(k + 1, count):
            lower[i, k] = work[i, k] * inverse[k]
        for i in range(k + 1, count):
            for j in range(k + 1, i + 1):
                work[i, j] = work[i, j] - lower[i, k] * work[j, k]
    return lower, inverse


def spd_solve(factor, right, count):
    lower, inverse = factor
    result = {}
    for column in range(count):
        values = [right[row, column] for row in range(count)]
        for i in range(count):
            for k in range(i):
                values[i] = values[i] - lower[i, k] * values[k]
        values = [value * scale for value, scale in zip(values, inverse)]
        for i in reversed(range(count)):
            for k in range(i + 1, count):
                values[i] = values[i] - lower[k, i] * values[k]
        for row in range(count):
            result[row, column] = values[row]
    return result


def kernel(
    sizes, stages,
    design, supports, body, start, nodes, values,
    solution_ref, residual_ref,
    field, rowtx, rowrx, coltx, colrx, movable_ref, scale_ref, modulus,
    resid, direct, image, second, second_image, grams, coef, sumtx, sumrx,
    halo_send, halo_recv, sum_send, sum_recv,
):
    cases, _, n0, n1, n2 = start.shape
    loads = nodes.shape[1]
    fields = 3 * cases
    rows, lanes = field.shape[-2:]
    corner_stiffness, modes = mode_matrix()
    place = {axis: lax.axis_index(axis) for axis in AXES}

    def present(d):
        inside = None
        for axis, step in zip(AXES, d):
            if step:
                test = (place[axis] > 0) if step < 0 else (place[axis] < sizes[axis] - 1)
                inside = test if inside is None else jnp.logical_and(inside, test)
        return inside

    def target(d):
        return {axis: place[axis] + step for axis, step in zip(AXES, d) if step}

    def possible(d):
        return all(step == 0 or sizes[axis] > 1 for axis, step in zip(AXES, d))

    directions = [d for d in DIRECTIONS if possible(d)]

    def members(stage):
        index, size = 0, 1
        for axis in stage:
            index = index * sizes[axis] + place[axis]
            size = size * sizes[axis]
        return index, size

    def peer(stage, number):
        out = {}
        for axis in reversed(stage):
            out[axis] = lax.rem(number, sizes[axis])
            number = lax.div(number, sizes[axis])
        return out

    barrier = pltpu.get_barrier_semaphore()
    if any(sizes[axis] > 1 for axis in AXES):
        rowrx[...] = jnp.zeros_like(rowrx)
        colrx[...] = jnp.zeros_like(colrx)
        for turn in range(3):
            zero = jnp.zeros((field.shape[1], 1, n1, n2), jnp.float32)
            field[turn, :, 0:1, 0:n1, 0:n2] = zero
            field[turn, :, n0 + 1 : n0 + 2, 0:n1, 0:n2] = zero
    expected = 0
    for stage in stages:
        index, size = members(stage)
        expected = expected + (size - 1)
        for offset in range(1, size):
            pl.semaphore_signal(
                barrier, inc=1, device_id=peer(stage, lax.rem(index + offset, size)), device_id_type=MESH
            )
    if len(stages) > 1:
        for d in directions:
            expected = expected + present(d).astype(jnp.int32)

            @pl.when(present(d))
            def _():
                pl.semaphore_signal(barrier, inc=1, device_id=target(d), device_id_type=MESH)

    lane = lax.broadcasted_iota(jnp.int32, (n1, 128), 1)
    row = lax.broadcasted_iota(jnp.int32, (8, n2), 0)

    def planes(step):
        if step == 0:
            return pl.ds(0, n0), pl.ds(1, n0)
        if step > 0:
            return pl.ds(n0 - 1, 1), pl.ds(0, 1)
        return pl.ds(0, 1), pl.ds(n0 + 1, 1)

    def opposite(d):
        return tuple(-step for step in d)

    def halo_copy(turn, number, count, toward=None):
        d = directions[number]
        source, goal = planes(d[0])
        if d[2]:
            side = 0 if d[2] > 0 else 1
            src = coltx.at[turn, side, source]
            dst = colrx.at[turn, side, 1 - d[1], goal]
        elif d[1]:
            side = 0 if d[1] > 0 else 1
            src = rowtx.at[turn, side, source]
            dst = rowrx.at[turn, side, goal]
        else:
            inner = pl.ds(n0 if d[0] > 0 else 1, 1)
            part = (turn, pl.ds(0, count))
            src = field.at[part + (inner, pl.ds(0, n1), pl.ds(0, n2))]
            dst = field.at[part + (goal, pl.ds(0, n1), pl.ds(0, n2))]
        return pltpu.make_async_remote_copy(
            src_ref=src, dst_ref=dst,
            send_sem=halo_send.at[turn, number], recv_sem=halo_recv.at[turn, number],
            device_id=target(toward or d), device_id_type=MESH,
        )

    def pack(turn, count):
        for p in range(n0):
            low = jnp.zeros((n1, 128), jnp.float32)
            high = jnp.zeros((n1, 128), jnp.float32)
            for f in range(count):
                block = field[turn, f, 1 + p, 0:n1, 0:n2]
                rowtx[turn, 0, p, f : f + 1, :] = block[n1 - 1 : n1]
                rowtx[turn, 1, p, f : f + 1, :] = block[0:1]
                high = jnp.where(lane == f, block[:, n2 - 1 : n2], high)
                low = jnp.where(lane == f, block[:, 0:1], low)
            coltx[turn, 0, p] = high
            coltx[turn, 1, p] = low

    def halo_start(turn, count):
        for number, d in enumerate(directions):
            @pl.when(present(d))
            def _():
                halo_copy(turn, number, count).start()

    def halo_finish(turn, count):
        for number, d in enumerate(directions):
            @pl.when(present(opposite(d)))
            def _():
                halo_copy(turn, number, count, opposite(d)).wait_recv()

        def unpack(q, carry):
            for f in range(count):
                low, high = rowrx[turn, 0, q, f : f + 1, :], rowrx[turn, 1, q, f : f + 1, :]
                field[turn, f, q, n1 : n1 + 8, 0:n2] = jnp.where(row == 0, high, jnp.where(row == 7, low, 0.0))
                for yy, top, size in ((1, 0, n1), (None, n1, 8)):
                    if yy is None:
                        first = colrx[turn, 1, 2, q, 0:1, f : f + 1]
                        last = colrx[turn, 1, 0, q, n1 - 1 : n1, f : f + 1]
                        after = jnp.where(row[:, 0:1] == 0, first, jnp.where(row[:, 0:1] == 7, last, 0.0))
                        first = colrx[turn, 0, 2, q, 0:1, f : f + 1]
                        last = colrx[turn, 0, 0, q, n1 - 1 : n1, f : f + 1]
                        before = jnp.where(row[:, 0:1] == 0, first, jnp.where(row[:, 0:1] == 7, last, 0.0))
                    else:
                        after = colrx[turn, 1, 1, q, :, f : f + 1]
                        before = colrx[turn, 0, 1, q, :, f : f + 1]
                    where = lane[0:1] if size != n1 else lane
                    field[turn, f, q, top : top + size, n2 : n2 + 128] = jnp.where(
                        where == 0, after, jnp.where(where == 127, before, 0.0)
                    )
            return carry

        lax.fori_loop(0, n0 + 2, unpack, 0)

    def sum_start(turn, step, tile):
        stage = stages[step]
        index, size = members(stage)
        sumtx[turn, step] = tile
        sumrx[turn, step, pl.ds(index, 1)] = tile[None]
        for offset in range(1, size):
            sum_copy(turn, step, offset).start()

    def sum_copy(turn, step, offset):
        stage = stages[step]
        index, size = members(stage)
        return pltpu.make_async_remote_copy(
            src_ref=sumtx.at[turn, step],
            dst_ref=sumrx.at[turn, step, index],
            send_sem=sum_send.at[turn, step, offset], recv_sem=sum_recv.at[turn, step, offset],
            device_id=peer(stage, lax.rem(index + offset, size)), device_id_type=MESH,
        )

    def sum_finish(turn):
        for step, stage in enumerate(stages):
            _, size = members(stage)
            for offset in range(1, size):
                sum_copy(turn, step, offset).wait_recv()
            total = sumrx[turn, step, 0]
            for number in range(1, size):
                total = total + sumrx[turn, step, number]
            if step + 1 < len(stages):
                sum_start(turn, step + 1, total)
        spots = lax.broadcasted_iota(jnp.int32, (grams.shape[0], 128), 0)
        across = lax.broadcasted_iota(jnp.int32, (grams.shape[0], 128), 1)
        spread = jnp.where(spots == across, total[0:1], 0.0)
        grams[...] = jnp.broadcast_to(jnp.sum(spread, axis=1, keepdims=True), grams.shape)

    def gram_rows(first, other, pairs, base):
        for number, (i, j) in enumerate(pairs):
            product = None
            for d in range(3):
                for p in range(n0):
                    term = first[i, d, p] * other[j, d, p]
                    product = term if product is None else product + term
            grams[base + number : base + number + 1, :] = jnp.sum(product, axis=0, keepdims=True)

    def gram_tile():
        return lax.dot_general(
            jnp.ones((8, 128), jnp.float32), grams[...], (((1,), (1,)), ((), ())),
            precision=lax.Precision.HIGHEST, preferred_element_type=jnp.float32,
        )

    def apply(turn, finish):
        def one(c, carry):
            def plane(q):
                parts = {}
                for d in range(3):
                    v = field[turn, 3 * c + d, q]
                    after = pltpu.roll(v, lanes - 1, 1)
                    for cc, along in enumerate((v + after, after - v)):
                        beyond = pltpu.roll(along, rows - 1, 0)
                        parts[d, 0, cc] = along + beyond
                        parts[d, 1, cc] = beyond - along
                return parts

            before, behind = plane(0), None
            for q in range(n0 + 1):
                ahead = plane(q + 1)
                strain = {}
                for d, b, cc in ahead:
                    strain[4 * 0 + 2 * b + cc, d] = ahead[d, b, cc] + before[d, b, cc]
                    strain[4 * 1 + 2 * b + cc, d] = ahead[d, b, cc] - before[d, b, cc]
                stiff = modulus[q]
                stress = {}
                for number in range(8):
                    for d in range(3):
                        total = None
                        for other in range(8):
                            for e in range(3):
                                weight = modes[3 * number + d, 3 * other + e]
                                if weight != 0.0:
                                    term = float(weight) * strain[other, e]
                                    total = term if total is None else total + term
                        stress[number, d] = None if total is None else total * stiff

                def side(sign):
                    out = {}
                    for d in range(3):
                        for b in range(2):
                            for cc in range(2):
                                total, change = stress[2 * b + cc, d], stress[4 + 2 * b + cc, d]
                                if total is None:
                                    out[d, b, cc] = change if sign > 0 else -change
                                else:
                                    out[d, b, cc] = total + change if sign > 0 else total - change
                    return out

                if q > 0:
                    near = side(-1)
                    for d in range(3):
                        folded = []
                        for cc in range(2):
                            flat = behind[d, 0, cc] + near[d, 0, cc]
                            tilt = behind[d, 1, cc] + near[d, 1, cc]
                            folded.append((flat - tilt)[0:n1] + pltpu.roll(flat + tilt, 1, 0)[0:n1])
                        force = (folded[0] - folded[1])[:, 0:n2]
                        force = force + pltpu.roll(folded[0] + folded[1], 1, 1)[:, 0:n2]
                        finish(c, d, q - 1, force)
                if q < n0:
                    behind = side(1)
                before = ahead
            return carry

        lax.fori_loop(0, cases, one, 0)

    for p in range(n0):
        density = (design[p].astype(jnp.float32) + 1.0) * (1.0 / LEVELS)
        movable_ref[p] = 1.0 - supports[p].astype(jnp.float32)
        field[0, fields, 1 + p, 0:n1, 0:n2] = soft_modulus + (1.0 - soft_modulus) * density * density * density
    for c in range(cases):
        for d in range(3):
            for p in range(n0):
                field[0, 3 * c + d, 1 + p, 0:n1, 0:n2] = movable_ref[p] * start[c, d, p]
    pack(0, fields + 1)
    pl.semaphore_wait(barrier, expected)
    halo_start(0, fields + 1)

    along1, along2 = n1 * sizes["gy"], n2 * sizes["gz"]

    def load_case(c, carry):
        for p in range(n0):
            first = place["gx"] * n0 + p
            second_index = place["gy"] * n1 + lax.broadcasted_iota(jnp.int32, (n1, n2), 0)
            third = place["gz"] * n2 + lax.broadcasted_iota(jnp.int32, (n1, n2), 1)
            number = (first * along1 + second_index) * along2 + third
            sums = [body[c, d, p] for d in range(3)]
            for l in range(loads):
                hit = number == nodes[c, l]
                for d in range(3):
                    sums[d] = sums[d] + jnp.where(hit, values[c, l * 3 + d], 0.0)
            for d in range(3):
                resid[c, d, p] = movable_ref[p] * sums[d]
        return carry

    lax.fori_loop(0, cases, load_case, 0)
    halo_finish(0, fields + 1)
    for q in range(n0 + 1):
        modulus[q] = field[0, fields, q]
    for p in range(n0):
        total = modulus[p] + modulus[p + 1]
        total = total + pltpu.roll(total, 1, 0)
        total = total + pltpu.roll(total, 1, 1)
        movable = movable_ref[p]
        guarded = jnp.where(movable > 0, total[0:n1, 0:n2], 1.0)
        scale_ref[p] = movable / (corner_stiffness * guarded) + (1.0 - movable)

    def first_finish(c, d, p, force):
        movable = movable_ref[p]
        value = resid[c, d, p] - (movable * force + (1.0 - movable) * start[c, d, p])
        resid[c, d, p] = value
        direction = scale_ref[p] * value
        direct[c, d, p] = direction
        field[1, 3 * c + d, 1 + p, 0:n1, 0:n2] = movable * direction

    apply(0, first_finish)
    pack(1, fields)
    halo_start(1, fields)
    pairs = triangle(cases)
    count = len(pairs)
    grams[...] = jnp.zeros_like(grams)
    gram_rows(direct, resid, pairs, count)
    halo_finish(1, fields)

    def second_finish(c, d, p, force):
        movable = movable_ref[p]
        value = movable * force + (1.0 - movable) * direct[c, d, p]
        image[c, d, p] = value
        scaled = scale_ref[p] * value
        second[c, d, p] = scaled
        field[2, 3 * c + d, 1 + p, 0:n1, 0:n2] = movable * scaled

    apply(1, second_finish)
    pack(2, fields)
    halo_start(2, fields)
    gram_rows(direct, image, pairs, 0)
    gram_rows(image, second, pairs, 2 * count)
    sum_start(0, 0, gram_tile())
    halo_finish(2, fields)

    def third_finish(c, d, p, force):
        movable = movable_ref[p]
        second_image[c, d, p] = movable * force + (1.0 - movable) * second[c, d, p]

    apply(2, third_finish)
    sum_finish(0)

    def entries(base):
        spot = {}
        for number, (i, j) in enumerate(pairs):
            spot[i, j] = spot[j, i] = base + number
        return lambda i, j: grams[spot[i, j] : spot[i, j] + 1, :]

    everyone = [(i, j) for i in range(cases) for j in range(cases)]
    curvature, projection, crossing = entries(0), entries(count), entries(2 * count)
    factor = spd_factor(curvature, cases)
    step = spd_solve(factor, {pair: projection(*pair) for pair in everyone}, cases)
    coupling = {}
    for i, j in everyone:
        total = curvature(j, i)
        for k in range(cases):
            total = total - crossing(i, k) * step[k, j]
        coupling[i, j] = total
    beta = spd_solve(factor, coupling, cases)
    for number, pair in enumerate(everyone):
        coef[0, number] = jnp.broadcast_to(step[pair], coef.shape[2:])
        coef[1, number] = jnp.broadcast_to(beta[pair], coef.shape[2:])

    def first_update(number, carry):
        d, p = lax.div(number, n0), lax.rem(number, n0)
        scale = scale_ref[p]
        for i in range(cases):
            gain, loss, kept, moved = start[i, d, p], resid[i, d, p], None, image[i, d, p]
            for j in range(cases):
                alpha, weight = coef[0, j * cases + i], coef[1, j * cases + i]
                gain = gain + direct[j, d, p] * alpha
                loss = loss - image[j, d, p] * alpha
                term = direct[j, d, p] * weight
                kept = term if kept is None else kept + term
                moved = moved - (second_image[j, d, p] * alpha + image[j, d, p] * weight)
            solution_ref[i, d, p] = gain
            residual_ref[i, d, p] = loss
            field[0, 3 * i + d, 1 + p, 0:n1, 0:n2] = scale * loss - kept
            field[1, 3 * i + d, 1 + p, 0:n1, 0:n2] = moved
        for i in range(cases):
            second[i, d, p] = field[0, 3 * i + d, 1 + p, 0:n1, 0:n2]
            second_image[i, d, p] = field[1, 3 * i + d, 1 + p, 0:n1, 0:n2]
        return carry

    halo_drain(halo_copy, directions, present, (0, 1, 2), fields)
    lax.fori_loop(0, 3 * n0, first_update, 0)
    grams[...] = jnp.zeros_like(grams)
    gram_rows(second, second_image, pairs, 0)
    gram_rows(second, residual_ref, everyone, count)
    sum_start(1, 0, gram_tile())
    sum_finish(1)
    curvature = entries(0)
    factor = spd_factor(curvature, cases)
    right = {pair: grams[count + n : count + n + 1, :] for n, pair in enumerate(everyone)}
    step = spd_solve(factor, right, cases)
    for number, pair in enumerate(everyone):
        coef[0, number] = jnp.broadcast_to(step[pair], coef.shape[2:])

    def second_update(number, carry):
        d, p = lax.div(number, n0), lax.rem(number, n0)
        for i in range(cases):
            gain, loss = solution_ref[i, d, p], residual_ref[i, d, p]
            for j in range(cases):
                alpha = coef[0, j * cases + i]
                gain = gain + second[j, d, p] * alpha
                loss = loss - second_image[j, d, p] * alpha
            solution_ref[i, d, p] = gain
            residual_ref[i, d, p] = loss
        return carry

    lax.fori_loop(0, 3 * n0, second_update, 0)
    for turn in range(2):
        for number, stage in enumerate(stages):
            _, size = members(stage)
            for offset in range(1, size):
                sum_copy(turn, number, offset).wait_send()


def halo_drain(halo_copy, directions, present, turns, fields):
    for turn in turns:
        for number, d in enumerate(directions):
            @pl.when(present(d))
            def _():
                halo_copy(turn, number, fields + 1 if turn == 0 else fields).wait_send()


def solution(mesh):
    sizes = {axis: mesh.shape[axis] for axis in AXES}
    group = sizes["gx"] * sizes["gy"] * sizes["gz"]
    stages = [AXES] if group <= 16 else [("gz",), ("gy",), ("gx",)]

    def shards(design, supports, body_load, start, load_nodes, load_values):
        cases, _, n0, n1, n2 = start.shape
        fields = 3 * cases
        padded = -(-(fields + 1) // 8) * 8
        directions = len([d for d in DIRECTIONS if all(s == 0 or sizes[a] > 1 for a, s in zip(AXES, d))])
        widest = max(int(np.prod([sizes[axis] for axis in stage])) for stage in stages)
        f32 = jnp.float32
        vmem, smem = pl.BlockSpec(memory_space=pltpu.VMEM), pl.BlockSpec(memory_space=pltpu.SMEM)
        block = pltpu.VMEM(start.shape, f32)
        gram_count = -(-max(3 * cases * (cases + 1) // 2, cases * (cases + 1) // 2 + cases * cases) // 128) * 128
        scratch = [
            pltpu.VMEM((3, fields + 1, n0 + 2, n1 + 8, n2 + 128), f32),
            pltpu.VMEM((3, 2, n0, padded, n2), f32),
            pltpu.VMEM((3, 2, n0 + 2, padded, n2), f32),
            pltpu.VMEM((3, 2, n0, n1, 128), f32),
            pltpu.VMEM((3, 2, 3, n0 + 2, n1, 128), f32),
            pltpu.VMEM((n0, n1, n2), f32),
            pltpu.VMEM((n0, n1, n2), f32),
            pltpu.VMEM((n0 + 1, n1 + 8, n2 + 128), f32),
            block, block, block, block, block,
            pltpu.VMEM((gram_count, 128), f32),
            pltpu.VMEM((2, cases * cases, n1, n2), f32),
            pltpu.VMEM((2, len(stages), 8, 128), f32),
            pltpu.VMEM((2, len(stages), widest, 8, 128), f32),
            pltpu.SemaphoreType.DMA((3, directions)),
            pltpu.SemaphoreType.DMA((3, directions)),
            pltpu.SemaphoreType.DMA((2, len(stages), widest)),
            pltpu.SemaphoreType.DMA((2, len(stages), widest)),
        ]
        return pl.pallas_call(
            functools.partial(kernel, sizes, stages),
            out_shape=(jax.ShapeDtypeStruct(start.shape, f32), jax.ShapeDtypeStruct(start.shape, f32)),
            in_specs=[vmem] * 4 + [smem] * 2,
            out_specs=(vmem, vmem),
            scratch_shapes=scratch,
            compiler_params=pltpu.CompilerParams(collective_id=0, has_side_effects=True),
        )(design, supports, body_load, start, load_nodes, load_values.reshape(cases, -1))

    in_specs = (
        P(("grp", "gx"), "gy", "gz"),
        P(("grp", "gx"), "gy", "gz"),
        P("grp", None, "gx", "gy", "gz"),
        P("grp", None, "gx", "gy", "gz"),
        P("grp", None),
        P("grp", None, None),
    )
    out_specs = (P("grp", None, "gx", "gy", "gz"), P("grp", None, "gx", "gy", "gz"))
    return jax.shard_map(shards, mesh=mesh, in_specs=in_specs, out_specs=out_specs, check_vma=False)
```

profile of v0, /device:TPU:0, one launch (start us, length us, event | category | flops | bytes accessed | tf_op | source)
XLA Modules:
  0.0 43.9 jit_solution(11992728026739700502)
XLA Ops:
  0.6 0.8 %copy.9 = f32[6,16,3]{2,1,0:T(8,128)S(1)} copy(f32[6,16,3]{1,2,0:T(4,128)} %param.11) | data formatting | bytes 2304 | tf_op args[5]
  1.4 0.7 %reshape.7.values = f32[6,48]{1,0:T(8,128)} reshape(f32[6,16,3]{2,1,0:T(8,128)S(1)} %copy.9) | data formatting | bytes 2304 | tf_op jit(solution)/shard_map/reshape | solution.py:576
  2.1 39.5 %shard_map.77 = (f32[6,3,2,8,128]{4,3,2,1,0:T(8,128)}, f32[6,3,2,8,128]{4,3,2,1,0:T(8,128)}) custom-call(s32[2,8,128]{2,1,0:T(8,128)} %design.1, s32[2,8,128]{2,1,0:T(8,128)} %supports.1, f32[6,3,2,8,128]{4,3,2,1,0:T(8,128)} %body.1, f32[6,3,2,8,128]{4,3,2,1,0:T(8,128)} %start.1, s32[6,16]{1,0:T(8,128)} %nodes.1, f32[6,48]{1,0:T(8,128)} %reshape.7.values), custom_call_target="tpu_custom_call" | custom-call | tf_op jit(solution)/shard_map/pallas_call | solution.py:569
  41.6 0.0 copy-start
  41.6 1.6 %copy.12 = f32[6,3,2,8,128]{4,3,2,1,0:T(8,128)} copy(f32[6,3,2,8,128]{4,3,2,1,0:T(8,128)} %get-tuple-element.4) | data formatting | bytes 294912
  43.2 0.0 copy-done
  43.2 0.7 %copy.13 = f32[6,3,2,8,128]{4,3,2,1,0:T(8,128)} copy(f32[6,3,2,8,128]{4,3,2,1,0:T(8,128)S(1)} %copy-done) | data formatting | bytes 294912
Async XLA Ops:
  41.6 1.6 %copy-start = (f32[6,3,2,8,128]{4,3,2,1,0:T(8,128)S(1)}, f32[6,3,2,8,128]{4,3,2,1,0:T(8,128)}, u32[]{:S(2)}) copy-start(f32[6,3,2,8,128]{4,3,2,1,0:T(8,128)} %get-tuple-element.5) | copy-start | bytes 442372
where the time goes:
time: 44.1 us; the launch traced here: 43.9 us
  Pallas kernels  39.5 us (90%)
  local copies, waits for them, and re-layouts  3.77 us (9%)
  between operations  0.65 us (1%)
    pallas_call x1, Pallas kernels, shards(): pl.pallas_call(functools.partial(kernel, sizes, stages), out_shape=(jax.S...  39.5 us
    unnamed x5, local copies, waits for them, and re-layouts  3.1 us

commit v1 on v0

--- a/solution.py
+++ b/solution.py
@@ -14,7 +14,12 @@
 MESH = pl.DeviceIdType.MESH
 soft_modulus = 0.05
 poisson_ratio = 0.3
-DIRECTIONS = [d for d in itertools.product((-1, 0, 1), repeat=3) if d != (0, 0, 0)]
+SWAP = 2
+
+
+def neighbours(sizes):
+    options = [(0,) if sizes[axis] == 1 else (0, SWAP) if sizes[axis] == 2 else (-1, 0, 1) for axis in AXES]
+    return [d for d in itertools.product(*options) if any(d)]
 
 
 def corner_list():
@@ -106,11 +111,11 @@
 
 def kernel(
     sizes, stages,
-    design, supports, body, start, nodes, values,
-    solution_ref, residual_ref,
+    design_hbm, supports_hbm, body_hbm, start_hbm, nodes, values,
+    solution_ref, residual_ref, design, supports, body, start,
     field, rowtx, rowrx, coltx, colrx, movable_ref, scale_ref, modulus,
     resid, direct, image, second, second_image, grams, coef, sumtx, sumrx,
-    halo_send, halo_recv, sum_send, sum_recv,
+    halo_send, halo_recv, sum_send, sum_recv, load_sem,
 ):
     cases, _, n0, n1, n2 = start.shape
     loads = nodes.shape[1]
@@ -122,18 +127,29 @@
     def present(d):
         inside = None
         for axis, step in zip(AXES, d):
-            if step:
+            if step in (-1, 1):
                 test = (place[axis] > 0) if step < 0 else (place[axis] < sizes[axis] - 1)
                 inside = test if inside is None else jnp.logical_and(inside, test)
         return inside
 
+    def when(condition, run):
+        if condition is None:
+            run()
+        else:
+            pl.when(condition)(run)
+
     def target(d):
-        return {axis: place[axis] + step for axis, step in zip(AXES, d) if step}
-
-    def possible(d):
-        return all(step == 0 or sizes[axis] > 1 for axis, step in zip(AXES, d))
-
-    directions = [d for d in DIRECTIONS if possible(d)]
+        return {
+            axis: 1 - place[axis] if step == SWAP else place[axis] + step
+            for axis, step in zip(AXES, d) if step
+        }
+
+    def opposite(d):
+        return tuple(step if step == SWAP else -step for step in d)
+
+    directions = neighbours(sizes)
+    faces = [d for d in directions if d[0] and not d[1] and not d[2]]
+    packed = [d for d in directions if d not in faces]
 
     def members(stage):
         index, size = 0, 1
@@ -149,6 +165,14 @@
             number = lax.div(number, sizes[axis])
         return out
 
+    loaded = [
+        pltpu.make_async_copy(source, goal, load_sem.at[number])
+        for number, (source, goal) in enumerate(
+            ((start_hbm, start), (supports_hbm, supports), (design_hbm, design), (body_hbm, body))
+        )
+    ]
+    for copy in loaded:
+        copy.start()
     barrier = pltpu.get_barrier_semaphore()
     if any(sizes[axis] > 1 for axis in AXES):
         rowrx[...] = jnp.zeros_like(rowrx)
@@ -167,11 +191,13 @@
             )
     if len(stages) > 1:
         for d in directions:
-            expected = expected + present(d).astype(jnp.int32)
-
-            @pl.when(present(d))
-            def _():
+            exists = present(d)
+            expected = expected + (1 if exists is None else exists.astype(jnp.int32))
+
+            def greet():
                 pl.semaphore_signal(barrier, inc=1, device_id=target(d), device_id_type=MESH)
+
+            when(exists, greet)
 
     lane = lax.broadcasted_iota(jnp.int32, (n1, 128), 1)
     row = lax.broadcasted_iota(jnp.int32, (8, n2), 0)
@@ -179,34 +205,50 @@
     def planes(step):
         if step == 0:
             return pl.ds(0, n0), pl.ds(1, n0)
+        if step == SWAP:
+            return pl.ds((n0 - 1) * (1 - place["gx"]), 1), pl.ds((n0 + 1) * place["gx"], 1)
         if step > 0:
             return pl.ds(n0 - 1, 1), pl.ds(0, 1)
         return pl.ds(0, 1), pl.ds(n0 + 1, 1)
 
-    def opposite(d):
-        return tuple(-step for step in d)
-
-    def halo_copy(turn, number, count, toward=None):
-        d = directions[number]
+    def side_of(axis, step):
+        return place[axis] if step == SWAP else (0 if step > 0 else 1)
+
+    def remote(turn, d, src, dst, toward):
+        number = directions.index(d)
+        return pltpu.make_async_remote_copy(
+            src_ref=src, dst_ref=dst,
+            send_sem=halo_send.at[number], recv_sem=halo_recv.at[turn, number],
+            device_id=target(toward or d), device_id_type=MESH,
+        )
+
+    def pack_copy(turn, d, toward=None):
         source, goal = planes(d[0])
         if d[2]:
-            side = 0 if d[2] > 0 else 1
+            side = side_of("gz", d[2])
+            level = 2 * place["gy"] if d[1] == SWAP else 1 - d[1]
             src = coltx.at[turn, side, source]
-            dst = colrx.at[turn, side, 1 - d[1], goal]
-        elif d[1]:
-            side = 0 if d[1] > 0 else 1
+            dst = colrx.at[turn, side, level, goal]
+        else:
+            side = side_of("gy", d[1])
             src = rowtx.at[turn, side, source]
             dst = rowrx.at[turn, side, goal]
+        return remote(turn, d, src, dst, toward)
+
+    def face_copy(turn, d, first, count, toward=None):
+        source, goal = planes(d[0])
+        if d[0] == SWAP:
+            inner = pl.ds(1 + (n0 - 1) * (1 - place["gx"]), 1)
         else:
             inner = pl.ds(n0 if d[0] > 0 else 1, 1)
-            part = (turn, pl.ds(0, count))
-            src = field.at[part + (inner, pl.ds(0, n1), pl.ds(0, n2))]
-            dst = field.at[part + (goal, pl.ds(0, n1), pl.ds(0, n2))]
-        return pltpu.make_async_remote_copy(
-            src_ref=src, dst_ref=dst,
-            send_sem=halo_send.at[turn, number], recv_sem=halo_recv.at[turn, number],
-            device_id=target(toward or d), device_id_type=MESH,
-        )
+        part = (turn, pl.ds(first, count))
+        src = field.at[part + (inner, pl.ds(0, n1), pl.ds(0, n2))]
+        dst = field.at[part + (goal, pl.ds(0, n1), pl.ds(0, n2))]
+        return remote(turn, d, src, dst, toward)
+
+    def face_start(turn, first, count):
+        for d in faces:
+            when(present(d), lambda: face_copy(turn, d, first, count).start())
 
     def pack(turn, count):
         for p in range(n0):
@@ -221,17 +263,19 @@
             coltx[turn, 0, p] = high
             coltx[turn, 1, p] = low
 
-    def halo_start(turn, count):
-        for number, d in enumerate(directions):
-            @pl.when(present(d))
-            def _():
-                halo_copy(turn, number, count).start()
+    def halo_start(turn):
+        for d in packed:
+            when(present(d), lambda: pack_copy(turn, d).start())
 
     def halo_finish(turn, count):
-        for number, d in enumerate(directions):
-            @pl.when(present(opposite(d)))
-            def _():
-                halo_copy(turn, number, count, opposite(d)).wait_recv()
+        for d in packed:
+            when(present(opposite(d)), lambda: pack_copy(turn, d, opposite(d)).wait_recv())
+        for d in faces:
+            when(present(opposite(d)), lambda: face_copy(turn, d, 0, count, opposite(d)).wait_recv())
+        for d in packed:
+            when(present(d), lambda: pack_copy(turn, d).wait_send())
+        for d in faces:
+            when(present(d), lambda: face_copy(turn, d, 0, count).wait_send())
 
         def unpack(q, carry):
             for f in range(count):
@@ -262,23 +306,29 @@
         sumtx[turn, step] = tile
         sumrx[turn, step, pl.ds(index, 1)] = tile[None]
         for offset in range(1, size):
-            sum_copy(turn, step, offset).start()
-
-    def sum_copy(turn, step, offset):
+            pltpu.make_async_remote_copy(
+                src_ref=sumtx.at[turn, step],
+                dst_ref=sumrx.at[turn, step, index],
+                send_sem=sum_send.at[turn, step], recv_sem=sum_recv.at[turn, step],
+                device_id=peer(stage, lax.rem(index + offset, size)), device_id_type=MESH,
+            ).start()
+
+    def sum_wait(turn, step):
         stage = stages[step]
         index, size = members(stage)
-        return pltpu.make_async_remote_copy(
-            src_ref=sumtx.at[turn, step],
-            dst_ref=sumrx.at[turn, step, index],
-            send_sem=sum_send.at[turn, step, offset], recv_sem=sum_recv.at[turn, step, offset],
-            device_id=peer(stage, lax.rem(index + offset, size)), device_id_type=MESH,
-        )
+        if size > 1:
+            whole = sumrx.at[turn, step, pl.ds(0, size - 1)]
+            return pltpu.make_async_remote_copy(
+                src_ref=whole, dst_ref=whole,
+                send_sem=sum_send.at[turn, step], recv_sem=sum_recv.at[turn, step],
+                device_id=peer(stage, lax.rem(index + 1, size)), device_id_type=MESH,
+            )
 
     def sum_finish(turn):
         for step, stage in enumerate(stages):
             _, size = members(stage)
-            for offset in range(1, size):
-                sum_copy(turn, step, offset).wait_recv()
+            if size > 1:
+                sum_wait(turn, step).wait_recv()
             total = sumrx[turn, step, 0]
             for number in range(1, size):
                 total = total + sumrx[turn, step, number]
@@ -304,7 +354,7 @@
             precision=lax.Precision.HIGHEST, preferred_element_type=jnp.float32,
         )
 
-    def apply(turn, finish):
+    def apply(turn, finish, after=None):
         def one(c, carry):
             def plane(q):
                 parts = {}
@@ -363,10 +413,14 @@
                 if q < n0:
                     behind = side(1)
                 before = ahead
+            if after is not None:
+                after(c)
             return carry
 
         lax.fori_loop(0, cases, one, 0)
 
+    for copy in loaded[:3]:
+        copy.wait()
     for p in range(n0):
         density = (design[p].astype(jnp.float32) + 1.0) * (1.0 / LEVELS)
         movable_ref[p] = 1.0 - supports[p].astype(jnp.float32)
@@ -377,7 +431,9 @@
                 field[0, 3 * c + d, 1 + p, 0:n1, 0:n2] = movable_ref[p] * start[c, d, p]
     pack(0, fields + 1)
     pl.semaphore_wait(barrier, expected)
-    halo_start(0, fields + 1)
+    halo_start(0)
+    face_start(0, 0, fields + 1)
+    loaded[3].wait()
 
     along1, along2 = n1 * sizes["gy"], n2 * sizes["gz"]
 
@@ -391,7 +447,7 @@
             for l in range(loads):
                 hit = number == nodes[c, l]
                 for d in range(3):
-                    sums[d] = sums[d] + jnp.where(hit, values[c, l * 3 + d], 0.0)
+                    sums[d] = sums[d] + jnp.where(hit, values[c, l, d], 0.0)
             for d in range(3):
                 resid[c, d, p] = movable_ref[p] * sums[d]
         return carry
@@ -416,9 +472,9 @@
         direct[c, d, p] = direction
         field[1, 3 * c + d, 1 + p, 0:n1, 0:n2] = movable * direction
 
-    apply(0, first_finish)
+    apply(0, first_finish, lambda c: face_start(1, 3 * c, 3))
     pack(1, fields)
-    halo_start(1, fields)
+    halo_start(1)
     pairs = triangle(cases)
     count = len(pairs)
     grams[...] = jnp.zeros_like(grams)
@@ -433,9 +489,9 @@
         second[c, d, p] = scaled
         field[2, 3 * c + d, 1 + p, 0:n1, 0:n2] = movable * scaled
 
-    apply(1, second_finish)
+    apply(1, second_finish, lambda c: face_start(2, 3 * c, 3))
     pack(2, fields)
-    halo_start(2, fields)
+    halo_start(2)
     gram_rows(direct, image, pairs, 0)
     gram_rows(image, second, pairs, 2 * count)
     sum_start(0, 0, gram_tile())
@@ -490,7 +546,6 @@
             second_image[i, d, p] = field[1, 3 * i + d, 1 + p, 0:n1, 0:n2]
         return carry
 
-    halo_drain(halo_copy, directions, present, (0, 1, 2), fields)
     lax.fori_loop(0, 3 * n0, first_update, 0)
     grams[...] = jnp.zeros_like(grams)
     gram_rows(second, second_image, pairs, 0)
@@ -520,16 +575,8 @@
     for turn in range(2):
         for number, stage in enumerate(stages):
             _, size = members(stage)
-            for offset in range(1, size):
-                sum_copy(turn, number, offset).wait_send()
-
-
-def halo_drain(halo_copy, directions, present, turns, fields):
-    for turn in turns:
-        for number, d in enumerate(directions):
-            @pl.when(present(d))
-            def _():
-                halo_copy(turn, number, fields + 1 if turn == 0 else fields).wait_send()
+            if size > 1:
+                sum_wait(turn, number).wait_send()
 
 
 def solution(mesh):
@@ -541,13 +588,17 @@
         cases, _, n0, n1, n2 = start.shape
         fields = 3 * cases
         padded = -(-(fields + 1) // 8) * 8
-        directions = len([d for d in DIRECTIONS if all(s == 0 or sizes[a] > 1 for a, s in zip(AXES, d))])
+        directions = max(len(neighbours(sizes)), 1)
         widest = max(int(np.prod([sizes[axis] for axis in stage])) for stage in stages)
         f32 = jnp.float32
         vmem, smem = pl.BlockSpec(memory_space=pltpu.VMEM), pl.BlockSpec(memory_space=pltpu.SMEM)
         block = pltpu.VMEM(start.shape, f32)
         gram_count = -(-max(3 * cases * (cases + 1) // 2, cases * (cases + 1) // 2 + cases * cases) // 128) * 128
         scratch = [
+            pltpu.VMEM((n0, n1, n2), jnp.int32),
+            pltpu.VMEM((n0, n1, n2), jnp.int32),
+            block,
+            block,
             pltpu.VMEM((3, fields + 1, n0 + 2, n1 + 8, n2 + 128), f32),
             pltpu.VMEM((3, 2, n0, padded, n2), f32),
             pltpu.VMEM((3, 2, n0 + 2, padded, n2), f32),
@@ -561,19 +612,20 @@
             pltpu.VMEM((2, cases * cases, n1, n2), f32),
             pltpu.VMEM((2, len(stages), 8, 128), f32),
             pltpu.VMEM((2, len(stages), widest, 8, 128), f32),
+            pltpu.SemaphoreType.DMA((directions,)),
             pltpu.SemaphoreType.DMA((3, directions)),
-            pltpu.SemaphoreType.DMA((3, directions)),
-            pltpu.SemaphoreType.DMA((2, len(stages), widest)),
-            pltpu.SemaphoreType.DMA((2, len(stages), widest)),
+            pltpu.SemaphoreType.DMA((2, len(stages))),
+            pltpu.SemaphoreType.DMA((2, len(stages))),
+            pltpu.SemaphoreType.DMA((4,)),
         ]
         return pl.pallas_call(
             functools.partial(kernel, sizes, stages),
             out_shape=(jax.ShapeDtypeStruct(start.shape, f32), jax.ShapeDtypeStruct(start.shape, f32)),
-            in_specs=[vmem] * 4 + [smem] * 2,
+            in_specs=[pl.BlockSpec(memory_space=pltpu.HBM)] * 4 + [smem] * 2,
             out_specs=(vmem, vmem),
             scratch_shapes=scratch,
             compiler_params=pltpu.CompilerParams(collective_id=0, has_side_effects=True),
-        )(design, supports, body_load, start, load_nodes, load_values.reshape(cases, -1))
+        )(design, supports, body_load, start, load_nodes, load_values)
 
     in_specs = (
         P(("grp", "gx"), "gy", "gz"),

time: 44.1 us -> 40.3 us (0.914)
  Pallas kernels: 39.5 us -> 35.6 us
    pallas_call x1, Pallas kernels: 39.5 us -> 35.6 us  [shards(): pl.pallas_call(functools.partial(kernel, sizes, stages), out_shape=(jax.S...]
    reshape x1 -> x0, local copies, waits for them, and re-layouts: 0.68 us -> none  [shards(): load_values.reshape(cases, -1)]
    unnamed x5, local copies, waits for them, and re-layouts: 3.1 us -> 3.71 us
where the time goes in v1:
time: 40.3 us; the launch traced here: 40 us
  Pallas kernels  35.6 us (88%)
  local copies, waits for them, and re-layouts  3.71 us (9%)
  between operations  0.65 us (2%)
    pallas_call x1, Pallas kernels, shards(): pl.pallas_call(functools.partial(kernel, sizes, stages), out_shape=(jax.S...  35.6 us
    unnamed x5, local copies, waits for them, and re-layouts  3.71 us

profile of v1, /device:TPU:0, one launch (start us, length us, event | category | flops | bytes accessed | tf_op | source)
XLA Modules:
  0.0 40.0 jit_solution(3899111188293506158)
XLA Ops:
  0.6 1.4 %copy.8.values = f32[6,16,3]{2,1,0:T(8,128)} copy(f32[6,16,3]{1,2,0:T(4,128)} %param.11) | data formatting | bytes 2304 | tf_op args[5]
  2.1 35.6 %shard_map.77 = (f32[6,3,2,8,128]{4,3,2,1,0:T(8,128)}, f32[6,3,2,8,128]{4,3,2,1,0:T(8,128)}) custom-call(s32[2,8,128]{2,1,0:T(8,128)} %design_hbm.1, s32[2,8,128]{2,1,0:T(8,128)} %supports_hbm.1, f32[6,3,2,8,128]{4,3,2,1,0:T(8,128)} %body_hbm.1, f32[6,3,2,8,128]{4,3,2,1,0:T(8,128)} %start_hbm.1, s32[6,16]{1,0:T(8,128)} %nodes.1, f32[6,16,3]{2,1,0:T(8,128)} %copy.8.values), custom_call_target="tpu_custom_call" | custom-call | tf_op jit(solution)/shard_map/pallas_call | solution.py:621
  37.7 0.0 copy-start
  37.7 1.6 %copy.11 = f32[6,3,2,8,128]{4,3,2,1,0:T(8,128)} copy(f32[6,3,2,8,128]{4,3,2,1,0:T(8,128)} %get-tuple-element.4) | data formatting | bytes 294912
  39.3 0.0 copy-done
  39.3 0.7 %copy.12 = f32[6,3,2,8,128]{4,3,2,1,0:T(8,128)} copy(f32[6,3,2,8,128]{4,3,2,1,0:T(8,128)S(1)} %copy-done) | data formatting | bytes 294912
Async XLA Ops:
  37.7 1.6 %copy-start = (f32[6,3,2,8,128]{4,3,2,1,0:T(8,128)S(1)}, f32[6,3,2,8,128]{4,3,2,1,0:T(8,128)}, u32[]{:S(2)}) copy-start(f32[6,3,2,8,128]{4,3,2,1,0:T(8,128)} %get-tuple-element.5) | copy-start | bytes 442372

commit v2 on v1

--- a/solution.py
+++ b/solution.py
@@ -270,35 +270,33 @@
     def halo_finish(turn, count):
         for d in packed:
             when(present(opposite(d)), lambda: pack_copy(turn, d, opposite(d)).wait_recv())
+        def unpack(q, carry):
+            edge = lax.broadcasted_iota(jnp.int32, (8, 128), 0)
+            across = lax.broadcasted_iota(jnp.int32, (8, 128), 1)
+            corners = [
+                jnp.where(
+                    edge == 0, colrx[turn, side, 2, q, 0:1, :],
+                    jnp.where(edge == 7, colrx[turn, side, 0, q, n1 - 1 : n1, :], 0.0),
+                )
+                for side in range(2)
+            ]
+            sides = [colrx[turn, side, 1, q] for side in range(2)]
+            for f in range(count):
+                low, high = rowrx[turn, 0, q, f : f + 1, :], rowrx[turn, 1, q, f : f + 1, :]
+                field[turn, f, q, n1 : n1 + 8, 0:n2] = jnp.where(row == 0, high, jnp.where(row == 7, low, 0.0))
+                for (before, after), where, top, size in ((sides, lane, 0, n1), (corners, across, n1, 8)):
+                    field[turn, f, q, top : top + size, n2 : n2 + 128] = jnp.where(
+                        where == 0, after[:, f : f + 1], jnp.where(where == 127, before[:, f : f + 1], 0.0)
+                    )
+            return carry
+
+        lax.fori_loop(0, n0 + 2, unpack, 0)
         for d in faces:
             when(present(opposite(d)), lambda: face_copy(turn, d, 0, count, opposite(d)).wait_recv())
         for d in packed:
             when(present(d), lambda: pack_copy(turn, d).wait_send())
         for d in faces:
             when(present(d), lambda: face_copy(turn, d, 0, count).wait_send())
-
-        def unpack(q, carry):
-            for f in range(count):
-                low, high = rowrx[turn, 0, q, f : f + 1, :], rowrx[turn, 1, q, f : f + 1, :]
-                field[turn, f, q, n1 : n1 + 8, 0:n2] = jnp.where(row == 0, high, jnp.where(row == 7, low, 0.0))
-                for yy, top, size in ((1, 0, n1), (None, n1, 8)):
-                    if yy is None:
-                        first = colrx[turn, 1, 2, q, 0:1, f : f + 1]
-                        last = colrx[turn, 1, 0, q, n1 - 1 : n1, f : f + 1]
-                        after = jnp.where(row[:, 0:1] == 0, first, jnp.where(row[:, 0:1] == 7, last, 0.0))
-                        first = colrx[turn, 0, 2, q, 0:1, f : f + 1]
-                        last = colrx[turn, 0, 0, q, n1 - 1 : n1, f : f + 1]
-                        before = jnp.where(row[:, 0:1] == 0, first, jnp.where(row[:, 0:1] == 7, last, 0.0))
-                    else:
-                        after = colrx[turn, 1, 1, q, :, f : f + 1]
-                        before = colrx[turn, 0, 1, q, :, f : f + 1]
-                    where = lane[0:1] if size != n1 else lane
-                    field[turn, f, q, top : top + size, n2 : n2 + 128] = jnp.where(
-                        where == 0, after, jnp.where(where == 127, before, 0.0)
-                    )
-            return carry
-
-        lax.fori_loop(0, n0 + 2, unpack, 0)
 
     def sum_start(turn, step, tile):
         stage = stages[step]
@@ -447,7 +445,7 @@
             for l in range(loads):
                 hit = number == nodes[c, l]
                 for d in range(3):
-                    sums[d] = sums[d] + jnp.where(hit, values[c, l, d], 0.0)
+                    sums[d] = sums[d] + jnp.where(hit, values[c, d, l], 0.0)
             for d in range(3):
                 resid[c, d, p] = movable_ref[p] * sums[d]
         return carry
@@ -625,7 +623,7 @@
             out_specs=(vmem, vmem),
             scratch_shapes=scratch,
             compiler_params=pltpu.CompilerParams(collective_id=0, has_side_effects=True),
-        )(design, supports, body_load, start, load_nodes, load_values)
+        )(design, supports, body_load, start, load_nodes, load_values.transpose(0, 2, 1))
 
     in_specs = (
         P(("grp", "gx"), "gy", "gz"),

time: 40.3 us -> 37.8 us (0.938)
  local copies, waits for them, and re-layouts: 3.71 us -> 2.28 us
  Pallas kernels: 35.6 us -> 34.6 us
    unnamed x5 -> x4, local copies, waits for them, and re-layouts: 3.71 us -> 2.28 us
    pallas_call x1, Pallas kernels: 35.6 us -> 34.6 us  [shards(): pl.pallas_call(functools.partial(kernel, sizes, stages), out_shape=(jax.S...]
where the time goes in v2:
time: 37.8 us; the launch traced here: 37.6 us
  Pallas kernels  34.6 us (92%)
  local copies, waits for them, and re-layouts  2.28 us (6%)
  between operations  0.65 us (2%)
    pallas_call x1, Pallas kernels, shards(): pl.pallas_call(functools.partial(kernel, sizes, stages), out_shape=(jax.S...  34.6 us
    unnamed x4, local copies, waits for them, and re-layouts  2.28 us

profile of v2, /device:TPU:0, one launch (start us, length us, event | category | flops | bytes accessed | tf_op | source)
XLA Modules:
  0.0 37.6 jit_solution(12823750081808134504)
XLA Ops:
  0.6 34.6 %shard_map.77 = (f32[6,3,2,8,128]{4,3,2,1,0:T(8,128)}, f32[6,3,2,8,128]{4,3,2,1,0:T(8,128)}) custom-call(s32[2,8,128]{2,1,0:T(8,128)} %design_hbm.1, s32[2,8,128]{2,1,0:T(8,128)} %supports_hbm.1, f32[6,3,2,8,128]{4,3,2,1,0:T(8,128)} %body_hbm.1, f32[6,3,2,8,128]{4,3,2,1,0:T(8,128)} %start_hbm.1, s32[6,16]{1,0:T(8,128)} %nodes.1, f32[6,3,16]{2,1,0:T(4,128)} %bitcast.1), custom_call_target="tpu_custom_call" | custom-call | tf_op jit(solution)/shard_map/pallas_call | solution.py:619
  35.3 0.0 copy-start
  35.3 1.6 %copy.10 = f32[6,3,2,8,128]{4,3,2,1,0:T(8,128)} copy(f32[6,3,2,8,128]{4,3,2,1,0:T(8,128)} %get-tuple-element.4) | data formatting | bytes 294912
  36.9 0.0 copy-done
  36.9 0.7 %copy.11 = f32[6,3,2,8,128]{4,3,2,1,0:T(8,128)} copy(f32[6,3,2,8,128]{4,3,2,1,0:T(8,128)S(1)} %copy-done) | data formatting | bytes 294912
Async XLA Ops:
  35.3 1.6 %copy-start = (f32[6,3,2,8,128]{4,3,2,1,0:T(8,128)S(1)}, f32[6,3,2,8,128]{4,3,2,1,0:T(8,128)}, u32[]{:S(2)}) copy-start(f32[6,3,2,8,128]{4,3,2,1,0:T(8,128)} %get-tuple-element.5) | copy-start | bytes 442372
